TPU v7x, 32 devices: a whole 2x2x4 slice. The times are simulated.
32 devices in a mesh: row: 8 (over z, core), col: 4 (over y, x).
Axes of the slice: x: 2, y: 2, z: 4, core: 2. Of those that a mesh axis runs over, the one named last changes fastest.
Arguments:
- ladder_ints: float32 [4928, 4928], P('row', 'col'), may hold values from -0.078125 to 0.078125
- amplitudes: float32 [4928, 1024], P('row', 'col'), may hold values from -6 to 6
- phase_map: int32 [8], replicated, may hold values from 0 to 7, each once
Outputs:
- ladder_term: float32 [4928, 1024], P('row', 'col')
Inputs may be any that keep to these rules, and one draw needn't show every extreme that they name: `phase_map`: each phase appears once.
All inputs are finite; a program needn't handle non-finite values.
Results may differ from a plain program's by a relative error of at most 0.000078.
Values sent between devices are 32-bit elements; how exact they have to be, the bound alone decides.
A program may use at most 320 MiB of HBM per device.

v0:
```python
import jax
import jax.numpy as jnp
from jax import lax
from jax.sharding import PartitionSpec as P


def per_device(ladder_ints, amplitudes, phase_map):
    phases = lax.axis_size("row")
    spread = lax.all_to_all(amplitudes, "col", split_axis=0, concat_axis=1, tiled=True)
    rows_each = spread.shape[0]
    piece = lax.all_gather(spread, "row", axis=0, tiled=True)
    count = piece.shape[0]
    position = jnp.arange(count, dtype=jnp.int32)
    source = position // rows_each
    within = position % rows_each
    columns = within * phases + jnp.take(phase_map, source)
    chosen = jnp.take(ladder_ints, columns, axis=1)
    partial_value = jnp.dot(
        chosen, piece, precision=lax.Precision.HIGHEST, preferred_element_type=jnp.float32
    )
    return lax.psum_scatter(partial_value, "col", scatter_dimension=1, tiled=True)


def solution(mesh):
    in_specs = (P("row", "col"), P("row", "col"), P())
    out_specs = P("row", "col")
    return jax.shard_map(
        per_device, mesh=mesh, in_specs=in_specs, out_specs=out_specs, check_vma=False
    )
```

profile of v0, /device:TPU:0, one launch (start us, length us, event | category | flops | bytes accessed | tf_op | source)
XLA Modules:
  0.0 142.9 jit_solution(8082048879229056640)
XLA Ops:
  6.5 0.0 all-gather.3.cloned.1.call-start
  6.5 1.2 all_to_all.14
  7.7 14.9 %all_to_all.19 = f32[4,154,256]{2,1,0:T(8,128)S(1)} all-to-all(f32[4,154,256]{2,1,0:T(8,128)S(1)} %all_to_all.14), channel_id=1, replica_groups=mesh['row'=8,'col'=4] {'col'}, dimensions={0} | all-to-all | bytes 1261568 | tf_op jit(solution)/shard_map/all_to_all | solution.py:9
  22.6 0.4 copy.8
  23.0 1.2 reshape.145
  24.2 0.0 all-gather.3.cloned.1.call-update
  24.2 0.0 copy-start.1
  24.2 0.0 reduce-scatter.2.cloned.1.call-start
  24.3 3.4 %copy.7 = f32[616,1232]{0,1:T(8,128)S(1)} copy(f32[616,1232]{1,0:T(8,128)} %param.3) | data formatting | bytes 6071296 | tf_op args[0]
  27.7 0.1 compare_reduce_fusion
  27.8 0.0 copy-done.1
  27.8 0.7 fusion.16
  28.5 4.4 %fusion.13 = s32[1232]{0:T(1024)S(1)} fusion(s32[]{:T(128)} %bitcast.1, s32[]{:T(128)} %bitcast.2, s32[]{:T(128)} %bitcast.3, s32[]{:T(128)} %bitcast.4, s32[]{:T(128)} %bitcast.5, s32[]{:T(128)} %bitcast.7, s32[]{:T(128)} %bitcast.6), kind=kLoop, calls=%fused_computation.38 | loop fusion | flops 28336 | bytes 4956 | tf_op jit(solution)/shard_map/jit(_take)/gather | solution.py:16
  32.9 0.7 compare_and_fusion
  33.5 0.1 fusion.14
  33.6 4.8 %gather_fusion = f32[1232,616]{1,0:T(8,128)} fusion(f32[616,1232]{0,1:T(8,128)S(1)} %copy.7, s32[2048]{0:T(1024)S(1)} %pad_clamp_fusion), kind=kCustom, calls=%fused_computation | custom fusion | bytes 6076224 | tf_op jit(solution)/shard_map/jit(_take)/gather | solution.py:17
  38.4 0.0 copy-start
  38.4 41.6 %all-gather.3.cloned.1.call-done = f32[8,154,1024]{2,1,0:T(8,128)} async-done(((f32[1,154,1024]{2,1,0:T(8,128)}), f32[8,154,1024]{2,1,0:T(8,128)}) %all-gather.3.cloned.1.call-update) | async-done | bytes 5046288 | tf_op jit(solution)/shard_map/all_gather | solution.py:11
  80.1 4.4 %reshape.146 = f32[1232,1024]{1,0:T(8,128)} reshape(f32[8,154,1024]{2,1,0:T(8,128)} %all-gather.3.cloned.1.call-done) | data formatting | bytes 10092544
  84.4 0.0 copy-done
  84.4 13.9 %fusion = f32[616,1024]{1,0:T(8,128)} fusion(f32[1232,1024]{1,0:T(8,128)} %reshape.146, f32[1232,616]{1,0:T(8,128)S(1)} %copy-done, pred[1232]{0:T(1024)(128)(4,1)S(1)} %get-tuple-element.5), kind=kOutput, calls=%fused_computation.1 | convolution fusion | flops 9326269440 | bytes 10606288 | tf_op jit(solution)/shard_map/dot_general | solution.py:18
  98.4 0.0 reduce-scatter.2.cloned.1.call-update
  98.4 37.7 %reduce-scatter.2.cloned.1.call-done = f32[616,256]{1,0:T(8,128)} async-done(((f32[616,1024]{1,0:T(8,128)}), f32[616,256]{1,0:T(8,128)}) %reduce-scatter.2.cloned.1.call-update) | async-done | bytes 630800 | tf_op jit(solution)/shard_map/reduce_scatter | solution.py:21
  (1 shorter events, 0.0 us)
Async XLA Ops:
  6.5 73.5 %all-gather.3.cloned.1.call-start = ((), (), s32[]{:S(2)}) async-start(), calls=%async_computation.3 | async-start | bytes 5898240 | tf_op jit(solution)/shard_map/all_gather | solution.py:11
  24.2 3.5 %copy-start.1 = (s32[8]{0:T(128)S(1)}, s32[8]{0:T(128)}, u32[]{:S(2)}) copy-start(s32[8]{0:T(128)} %param.5) | copy-start | bytes 100
  24.2 111.8 %reduce-scatter.2.cloned.1.call-start = ((), (), s32[]{:S(2)}) async-start(), calls=%async_computation.2 | async-start | bytes 3153920 | tf_op jit(solution)/shard_map/reduce_scatter | solution.py:21
  38.4 46.0 %copy-start = (f32[1232,616]{1,0:T(8,128)S(1)}, f32[1232,616]{1,0:T(8,128)}, u32[]{:S(2)}) copy-start(f32[1232,616]{1,0:T(8,128)} %gather_fusion) | copy-start | bytes 9106948
Sparse Core Ops, SparseCore 0:
  24.3 55.6 all-gather.2
  98.5 37.4 reduce-scatter.1
where the time goes:
time: 143 us
  waiting for transfers between devices  79.3 us (55%)
  local copies, waits for them, and re-layouts  16 us (11%)
  blocking collectives  14.9 us (10%)
  matrix products  13.9 us (10%)
  between operations  13.5 us (9%)
  other arithmetic  5.18 us (4%)
    all_gather x1, waiting for transfers between devices, per_device(): piece = lax.all_gather(spread, 'row', axis=0, tiled=True)  41.6 us
    reduce_scatter x1, waiting for transfers between devices, per_device(): lax.psum_scatter(partial_value, 'col', scatter_dimension=1, tiled=True)  37.7 us
    all_to_all x1, blocking collectives, per_device(): lax.all_to_all(amplitudes, 'col', split_axis=0, concat_axis=1, tiled=True)  14.9 us
    dot_general x1, matrix products, per_device(): jnp.dot(chosen, piece, precision=lax.Precision.HIGHEST, preferred_element...  13.9 us
    unnamed x7, local copies, waits for them, and re-layouts  8.95 us
    gather x1, local copies, waits for them, and re-layouts, per_device(): chosen = jnp.take(ladder_ints, columns, axis=1)  4.83 us
    gather x2, other arithmetic, per_device(): columns = within * phases + jnp.take(phase_map, source)  4.45 us
  transfers between devices with their start and end apart: 2, of which 2 were waited for; matrix products, arithmetic and copies ran while one was open for 10% of the time, Pallas kernels for 0%

commit v1 on v0

v1 whole, which is shorter than its diff:
```python
import functools

import jax
import jax.numpy as jnp
from jax import lax
from jax.experimental import pallas as pl
from jax.experimental.pallas import tpu as pltpu
from jax.sharding import PartitionSpec as P

LANES = 128
GROUP = 256
MESH = pl.DeviceIdType.MESH


def flipped(index, mask, size):
    value, bit = 0, 1
    while bit < size:
        value = value + bit * (((index // bit) % 2 + (mask // bit) % 2) % 2)
        bit *= 2
    return value


def split(value):
    high = value.astype(jnp.bfloat16)
    return high, (value - high.astype(jnp.float32)).astype(jnp.bfloat16)


def kernel(
    n_row, n_col, halves, phase_ref, v_hbm, a_ref, out_ref,
    v_buf, v_high, v_low, perm, t_cat, blocks, partial, arrived,
    v_sem, block_sem, spread_sem, core_sem, up_sem, down_sem, partial_send, partial_recv,
):
    row, col = lax.axis_index("row"), lax.axis_index("col")
    line = n_row // 2
    chip, core = row // 2, row % 2
    other = chip * 2 + (1 - core)
    up, down = row + 2, row - 2
    has_up, has_down = chip < line - 1, chip > 0
    chunks = n_col * halves
    away = chunks - halves
    rows_each = blocks.shape[2]
    tiles, tile, depth = v_high.shape
    width = v_hbm.shape[1]
    per_group = GROUP // n_row

    def chunk_owner(t):
        return flipped(col, n_col - 1 - t // halves, n_col)

    def load_v(at):
        return pltpu.make_async_copy(v_hbm.at[pl.ds(at * tile, tile)], v_buf, v_sem)

    load_v(0).start()

    barrier = pltpu.get_barrier_semaphore()
    for mask in range(1, n_col):
        pl.semaphore_signal(
            barrier, inc=1, device_id=(row, flipped(col, mask, n_col)), device_id_type=MESH
        )
    pl.semaphore_signal(barrier, inc=1, device_id=(other, col), device_id_type=MESH)

    @pl.when(has_up)
    def _():
        pl.semaphore_signal(barrier, inc=1, device_id=(up, col), device_id_type=MESH)

    @pl.when(has_down)
    def _():
        pl.semaphore_signal(barrier, inc=1, device_id=(down, col), device_id_type=MESH)

    pl.semaphore_wait(barrier, n_col + has_up.astype(jnp.int32) + has_down.astype(jnp.int32))

    def spread(t):
        peer = chunk_owner(t)
        return pltpu.make_async_remote_copy(
            src_ref=a_ref.at[peer, t % halves],
            dst_ref=blocks.at[t, row],
            send_sem=spread_sem.at[t],
            recv_sem=block_sem.at[t, row],
            device_id=(row, peer),
            device_id_type=MESH,
        )

    def keep(t):
        return pltpu.make_async_copy(
            a_ref.at[col, t % halves], blocks.at[t, row], block_sem.at[t, row]
        )

    for t in range(away):
        spread(t).start()
    for t in range(away, chunks):
        keep(t).start()

    lane = lax.broadcasted_iota(jnp.int32, (GROUP, GROUP), 1)
    wanted = (lane % per_group) * n_row
    owner = lane // per_group
    for r in range(n_row):
        wanted = wanted + jnp.where(owner == r, phase_ref[r], 0)
    source = lax.broadcasted_iota(jnp.int32, (GROUP, GROUP), 0)
    perm[...] = jnp.where(source == wanted, 1.0, 0.0).astype(jnp.bfloat16)
    t_cat[...] = jnp.zeros_like(t_cat)

    def pass_on(t, block, sem, target):
        pltpu.make_async_remote_copy(
            src_ref=blocks.at[t, block],
            dst_ref=blocks.at[t, block],
            send_sem=sem,
            recv_sem=block_sem.at[t, block],
            device_id=(target, col),
            device_id_type=MESH,
        ).start()

    def await_block(t, block):
        pltpu.make_async_copy(
            blocks.at[t, block], blocks.at[t, block], block_sem.at[t, block]
        ).wait()

    def regroup(at):
        load_v(at).wait()

        def place(columns, kept):
            high, low = split(v_buf[:, columns])
            moves = perm[:kept, :]
            for to, part in ((v_high, high), (v_low, low)):
                moved = jnp.dot(part, moves, preferred_element_type=jnp.float32)
                yield to, moved.astype(jnp.bfloat16)

        full = width // GROUP

        @pl.loop(0, full)
        def _(g):
            columns = pl.ds(pl.multiple_of(g * GROUP, GROUP), GROUP)
            for to, moved in place(columns, GROUP):
                to[at, :, columns] = moved

        if width % GROUP:
            for to, moved in place(pl.ds(full * GROUP, width % GROUP), width % GROUP):
                to[at, :, full * GROUP:] = moved

    def multiply(t):
        @pl.loop(0, n_row)
        def _(r):
            for g in range(depth // GROUP):
                first = g * per_group
                count = min(per_group, rows_each - first)
                high, low = split(blocks[t, r, first:first + count, :])
                at = pl.ds(pl.multiple_of(g * GROUP + r * per_group, per_group), count)
                t_cat[at, :LANES] = high
                t_cat[at, LANES:] = low

        for at in range(tiles):
            both = jnp.dot(v_high[at], t_cat[...], preferred_element_type=jnp.float32)
            rest = jnp.dot(v_low[at], t_cat[:, :LANES], preferred_element_type=jnp.float32)
            partial[t, at * tile:(at + 1) * tile, :] = both[:, :LANES] + (both[:, LANES:] + rest)

    def give(t):
        return pltpu.make_async_remote_copy(
            src_ref=partial.at[t],
            dst_ref=arrived.at[t],
            send_sem=partial_send.at[t],
            recv_sem=partial_recv.at[t],
            device_id=(row, chunk_owner(t)),
            device_id_type=MESH,
        )

    @pl.loop(0, chunks + line - 1)
    def _(s):
        @pl.when(s < chunks)
        def _():
            await_block(s, row)

            @pl.when(has_up)
            def _():
                pass_on(s, row, up_sem, up)

            @pl.when(has_down)
            def _():
                pass_on(s, row, down_sem, down)

            pass_on(s, row, core_sem, other)

        @pl.when(s == 0)
        def _():
            for at in range(tiles):
                if at:
                    load_v(at).start()
                regroup(at)

        for far in range(1, line):
            t = s - far

            @pl.when((t >= 0) & (t < chunks))
            def _():
                @pl.when(chip >= far)
                def _():
                    block = row - 2 * far
                    await_block(t, block)

                    @pl.when(has_up)
                    def _():
                        pass_on(t, block, up_sem, up)

                    pass_on(t, block, core_sem, other)

                @pl.when(chip + far < line)
                def _():
                    block = row + 2 * far
                    await_block(t, block)

                    @pl.when(has_down)
                    def _():
                        pass_on(t, block, down_sem, down)

                    pass_on(t, block, core_sem, other)

        done = s - (line - 1)

        @pl.when(done >= 0)
        def _():
            for j in range(line):
                await_block(done, j * 2 + (1 - core))
            multiply(done)

            @pl.when(done < away)
            def _():
                give(done).start()

    for t in range(away):
        give(t).wait_recv()
    for h in range(halves):
        total = partial[away + h]
        for t in range(h, away, halves):
            total = total + arrived[t]
        out_ref[:, h * LANES:(h + 1) * LANES] = total

    def await_sent(sem, count):
        sent = blocks.at[:, pl.ds(0, count)]
        pltpu.make_async_copy(sent, sent, sem).wait()

    for t in range(away):
        give(t).wait_send()
        spread(t).wait_send()
    await_sent(core_sem, line)
    for at in range(line - 1):
        @pl.when(chip == at)
        def _():
            await_sent(up_sem, at + 1)

        @pl.when(chip == line - 1 - at)
        def _():
            await_sent(down_sem, at + 1)


def per_device(n_row, n_col, ladder_ints, amplitudes, phase_map):
    rows, width = ladder_ints.shape
    block, own = amplitudes.shape
    rows_each, halves = block // n_col, own // LANES
    chunks = n_col * halves
    depth = -(-width // GROUP) * GROUP
    tile = max(m for m in range(8, 641, 8) if rows % m == 0)
    tiles = rows // tile
    pieces = amplitudes.reshape(n_col, rows_each, halves, LANES).transpose(0, 2, 1, 3)
    dma = pltpu.SemaphoreType.DMA
    return pl.pallas_call(
        functools.partial(kernel, n_row, n_col, halves),
        out_shape=jax.ShapeDtypeStruct((rows, own), jnp.float32),
        in_specs=[
            pl.BlockSpec(memory_space=pltpu.SMEM),
            pl.BlockSpec(memory_space=pl.ANY),
            pl.BlockSpec(memory_space=pltpu.VMEM),
        ],
        out_specs=pl.BlockSpec(memory_space=pltpu.VMEM),
        scratch_shapes=[
            pltpu.VMEM((tile, width), jnp.float32),
            pltpu.VMEM((tiles, tile, depth), jnp.bfloat16),
            pltpu.VMEM((tiles, tile, depth), jnp.bfloat16),
            pltpu.VMEM((GROUP, GROUP), jnp.bfloat16),
            pltpu.VMEM((depth, 2 * LANES), jnp.bfloat16),
            pltpu.VMEM((chunks, n_row, rows_each, LANES), jnp.float32),
            pltpu.VMEM((chunks, rows, LANES), jnp.float32),
            pltpu.VMEM((chunks - halves, rows, LANES), jnp.float32),
            dma,
            dma((chunks, n_row)),
            dma((chunks - halves,)),
            dma,
            dma,
            dma,
            dma((chunks - halves,)),
            dma((chunks - halves,)),
        ],
        compiler_params=pltpu.CompilerParams(
            collective_id=0, has_side_effects=True, vmem_limit_bytes=67043328
        ),
    )(phase_map, ladder_ints, pieces)


def solution(mesh):
    in_specs = (P("row", "col"), P("row", "col"), P())
    out_specs = P("row", "col")
    return jax.shard_map(
        functools.partial(per_device, mesh.shape["row"], mesh.shape["col"]),
        mesh=mesh, in_specs=in_specs, out_specs=out_specs, check_vma=False,
    )
```

time: 143 us -> 66.1 us (0.46)
  waiting for transfers between devices: 79.3 us -> 0 us
  Pallas kernels: 0 us -> 61.6 us
  blocking collectives: 14.9 us -> 0 us
  matrix products: 13.9 us -> 0 us
  between operations: 13.5 us -> 0.01 us
  local copies, waits for them, and re-layouts: 16 us -> 4.22 us
  other arithmetic: 5.18 us -> 0 us
    pallas_call x0 -> x1, Pallas kernels: none -> 61.6 us  [per_device(): pl.pallas_call(functools.partial(kernel, n_row, n_col, halves), out_shape...]
    all_gather x1 -> x0, waiting for transfers between devices: 41.6 us -> none  [per_device(): piece = lax.all_gather(spread, 'row', axis=0, tiled=True)]
    reduce_scatter x1 -> x0, waiting for transfers between devices: 37.7 us -> none  [per_device(): lax.psum_scatter(partial_value, 'col', scatter_dimension=1, tiled=True)]
    all_to_all x1 -> x0, blocking collectives: 14.9 us -> none  [per_device(): lax.all_to_all(amplitudes, 'col', split_axis=0, concat_axis=1, tiled=True)]
    dot_general x1 -> x0, matrix products: 13.9 us -> none  [per_device(): jnp.dot(chosen, piece, precision=lax.Precision.HIGHEST, preferred_element...]
    unnamed x7 -> x1, local copies, waits for them, and re-layouts: 8.95 us -> 1.95 us
    gather x2 -> x0, local copies, waits for them, and re-layouts: 5.51 us -> none  [the longest x1 4.83 us: per_device(): chosen = jnp.take(ladder_ints, columns, axis=1)]
    gather x3 -> x0, other arithmetic: 4.46 us -> none  [the longest x2 4.45 us: per_device(): columns = within * phases + jnp.take(phase_map, source)]
  transfers between devices with their start and end apart: 2 -> 0, of which waited for: 2 -> 0; matrix products, arithmetic and copies ran while one was open for 10% -> 0% of each run, Pallas kernels for 0% -> 0%
where the time goes in v1:
time: 66.1 us; the launch traced here: 65.8 us
  Pallas kernels  61.6 us (93%)
  local copies, waits for them, and re-layouts  4.22 us (6%)
    pallas_call x1, Pallas kernels, per_device(): pl.pallas_call(functools.partial(kernel, n_row, n_col, halves), out_shape...  61.6 us
    reshape x2, local copies, waits for them, and re-layouts, per_device(): amplitudes.reshape(n_col, rows_each, halves, LANES).transpose(0, 2, 1, 3)  2.27 us
    unnamed x1, local copies, waits for them, and re-layouts  1.95 us

profile of v1, /device:TPU:0, one launch (start us, length us, event | category | flops | bytes accessed | tf_op | source)
XLA Modules:
  0.0 65.8 jit_solution(16491029595854631010)
XLA Ops:
  0.0 1.4 %reshape.3 = f32[4,154,2,128]{3,2,1,0:T(2,128)S(1)} reshape(f32[616,256]{1,0:T(8,128)} %param.4) | data formatting | bytes 1261568 | tf_op jit(solution)/shard_map/reshape | solution.py:260
  1.4 0.9 %copy.6 = f32[4,154,2,128]{3,1,2,0:T(8,128)} copy(f32[4,154,2,128]{3,2,1,0:T(2,128)S(1)} %reshape.3) | data formatting | bytes 1261568 | tf_op jit(solution)/shard_map/reshape | solution.py:260
  2.3 61.6 %shard_map.37 = f32[616,256]{1,0:T(8,128)} custom-call(s32[8]{0:T(128)} %phase_ref.1, f32[616,1232]{1,0:T(8,128)} %v_hbm.1, f32[4,2,154,128]{3,2,1,0:T(8,128)} %bitcast.3), custom_call_target="tpu_custom_call" | custom-call | tf_op jit(solution)/shard_map/pallas_call | solution.py:262
  63.9 1.9 %copy.8 = f32[616,256]{1,0:T(8,128)} copy(f32[616,256]{1,0:T(8,128)} %shard_map.37) | data formatting | bytes 1261568

commit v2 on v1

--- a/solution.py
+++ b/solution.py
@@ -9,6 +9,7 @@
 
 LANES = 128
 GROUP = 256
+LEAD = 1
 MESH = pl.DeviceIdType.MESH
 
 
@@ -26,9 +27,9 @@
 
 
 def kernel(
-    n_row, n_col, halves, phase_ref, v_hbm, a_ref, out_ref,
-    v_buf, v_high, v_low, perm, t_cat, blocks, partial, arrived,
-    v_sem, block_sem, spread_sem, core_sem, up_sem, down_sem, partial_send, partial_recv,
+    n_row, n_col, halves, phase_ref, v_hbm, a_hbm, out_ref,
+    v_buf, v_high, v_low, perm, t_cat, a_buf, pieces, blocks, partial, arrived,
+    v_sem, a_sem, block_sem, spread_sem, core_sem, up_sem, down_sem, partial_send, partial_recv,
 ):
     row, col = lax.axis_index("row"), lax.axis_index("col")
     line = n_row // 2
@@ -49,6 +50,8 @@
     def load_v(at):
         return pltpu.make_async_copy(v_hbm.at[pl.ds(at * tile, tile)], v_buf, v_sem)
 
+    load_a = pltpu.make_async_copy(a_hbm, a_buf, a_sem)
+    load_a.start()
     load_v(0).start()
 
     barrier = pltpu.get_barrier_semaphore()
@@ -66,12 +69,17 @@
     def _():
         pl.semaphore_signal(barrier, inc=1, device_id=(down, col), device_id_type=MESH)
 
+    load_a.wait()
+    for c in range(n_col):
+        for h in range(halves):
+            pieces[c, h] = a_buf[c * rows_each:(c + 1) * rows_each, h * LANES:(h + 1) * LANES]
+
     pl.semaphore_wait(barrier, n_col + has_up.astype(jnp.int32) + has_down.astype(jnp.int32))
 
     def spread(t):
         peer = chunk_owner(t)
         return pltpu.make_async_remote_copy(
-            src_ref=a_ref.at[peer, t % halves],
+            src_ref=pieces.at[peer, t % halves],
             dst_ref=blocks.at[t, row],
             send_sem=spread_sem.at[t],
             recv_sem=block_sem.at[t, row],
@@ -81,12 +89,34 @@
 
     def keep(t):
         return pltpu.make_async_copy(
-            a_ref.at[col, t % halves], blocks.at[t, row], block_sem.at[t, row]
+            pieces.at[col, t % halves], blocks.at[t, row], block_sem.at[t, row]
         )
+
+    def pass_on(t, block, sem, target, source=None):
+        pltpu.make_async_remote_copy(
+            src_ref=blocks.at[t, block] if source is None else source,
+            dst_ref=blocks.at[t, block],
+            send_sem=sem,
+            recv_sem=block_sem.at[t, block],
+            device_id=(target, col),
+            device_id_type=MESH,
+        ).start()
+
+    def pass_own(t, source=None):
+        @pl.when(has_up)
+        def _():
+            pass_on(t, row, up_sem, up, source)
+
+        @pl.when(has_down)
+        def _():
+            pass_on(t, row, down_sem, down, source)
+
+        pass_on(t, row, core_sem, other, source)
 
     for t in range(away):
         spread(t).start()
     for t in range(away, chunks):
+        pass_own(t, pieces.at[col, t % halves])
         keep(t).start()
 
     lane = lax.broadcasted_iota(jnp.int32, (GROUP, GROUP), 1)
@@ -97,16 +127,6 @@
     source = lax.broadcasted_iota(jnp.int32, (GROUP, GROUP), 0)
     perm[...] = jnp.where(source == wanted, 1.0, 0.0).astype(jnp.bfloat16)
     t_cat[...] = jnp.zeros_like(t_cat)
-
-    def pass_on(t, block, sem, target):
-        pltpu.make_async_remote_copy(
-            src_ref=blocks.at[t, block],
-            dst_ref=blocks.at[t, block],
-            send_sem=sem,
-            recv_sem=block_sem.at[t, block],
-            device_id=(target, col),
-            device_id_type=MESH,
-        ).start()
 
     def await_block(t, block):
         pltpu.make_async_copy(
@@ -161,23 +181,17 @@
             device_id_type=MESH,
         )
 
-    @pl.loop(0, chunks + line - 1)
+    @pl.loop(0, chunks + LEAD + line - 1)
     def _(s):
         @pl.when(s < chunks)
         def _():
             await_block(s, row)
 
-            @pl.when(has_up)
-            def _():
-                pass_on(s, row, up_sem, up)
-
-            @pl.when(has_down)
-            def _():
-                pass_on(s, row, down_sem, down)
-
-            pass_on(s, row, core_sem, other)
-
-        @pl.when(s == 0)
+        @pl.when(s < away)
+        def _():
+            pass_own(s)
+
+        @pl.when(s == LEAD)
         def _():
             for at in range(tiles):
                 if at:
@@ -185,7 +199,7 @@
                 regroup(at)
 
         for far in range(1, line):
-            t = s - far
+            t = s - LEAD - far
 
             @pl.when((t >= 0) & (t < chunks))
             def _():
@@ -211,7 +225,7 @@
 
                     pass_on(t, block, core_sem, other)
 
-        done = s - (line - 1)
+        done = s - LEAD - (line - 1)
 
         @pl.when(done >= 0)
         def _():
@@ -257,15 +271,15 @@
     depth = -(-width // GROUP) * GROUP
     tile = max(m for m in range(8, 641, 8) if rows % m == 0)
     tiles = rows // tile
-    pieces = amplitudes.reshape(n_col, rows_each, halves, LANES).transpose(0, 2, 1, 3)
+    spare = 4 * rows * own * 5 // 4
     dma = pltpu.SemaphoreType.DMA
     return pl.pallas_call(
         functools.partial(kernel, n_row, n_col, halves),
         out_shape=jax.ShapeDtypeStruct((rows, own), jnp.float32),
         in_specs=[
             pl.BlockSpec(memory_space=pltpu.SMEM),
-            pl.BlockSpec(memory_space=pl.ANY),
-            pl.BlockSpec(memory_space=pltpu.VMEM),
+            pl.BlockSpec(memory_space=pltpu.HBM),
+            pl.BlockSpec(memory_space=pltpu.HBM),
         ],
         out_specs=pl.BlockSpec(memory_space=pltpu.VMEM),
         scratch_shapes=[
@@ -274,9 +288,12 @@
             pltpu.VMEM((tiles, tile, depth), jnp.bfloat16),
             pltpu.VMEM((GROUP, GROUP), jnp.bfloat16),
             pltpu.VMEM((depth, 2 * LANES), jnp.bfloat16),
+            pltpu.VMEM((block, own), jnp.float32),
+            pltpu.VMEM((n_col, halves, rows_each, LANES), jnp.float32),
             pltpu.VMEM((chunks, n_row, rows_each, LANES), jnp.float32),
             pltpu.VMEM((chunks, rows, LANES), jnp.float32),
             pltpu.VMEM((chunks - halves, rows, LANES), jnp.float32),
+            dma,
             dma,
             dma((chunks, n_row)),
             dma((chunks - halves,)),
@@ -287,9 +304,9 @@
             dma((chunks - halves,)),
         ],
         compiler_params=pltpu.CompilerParams(
-            collective_id=0, has_side_effects=True, vmem_limit_bytes=67043328
+            collective_id=0, has_side_effects=True, vmem_limit_bytes=67043328 - spare
         ),
-    )(phase_map, ladder_ints, pieces)
+    )(phase_map, ladder_ints, amplitudes)
 
 
 def solution(mesh):

time: 66.1 us -> 61.8 us (0.935)
  local copies, waits for them, and re-layouts: 4.22 us -> 1.95 us
  Pallas kernels: 61.6 us -> 59.7 us
    reshape x2 -> x0, local copies, waits for them, and re-layouts: 2.27 us -> none  [per_device(): amplitudes.reshape(n_col, rows_each, halves, LANES).transpose(0, 2, 1, 3)]
    pallas_call x1, Pallas kernels: 61.6 us -> 59.7 us  [per_device(): pl.pallas_call(functools.partial(kernel, n_row, n_col, halves), out_shape...]
where the time goes in v2:
time: 61.8 us; the launch traced here: 61.6 us
  Pallas kernels  59.7 us (97%)
  local copies, waits for them, and re-layouts  1.95 us (3%)
    pallas_call x1, Pallas kernels, per_device(): pl.pallas_call(functools.partial(kernel, n_row, n_col, halves), out_shape...  59.7 us
    unnamed x1, local copies, waits for them, and re-layouts  1.95 us

profile of v2, /device:TPU:0, one launch (start us, length us, event | category | flops | bytes accessed | tf_op | source)
XLA Modules:
  0.0 61.6 jit_solution(16947825628146556250)
XLA Ops:
  0.0 59.7 %shard_map.37 = f32[616,256]{1,0:T(8,128)} custom-call(s32[8]{0:T(128)} %phase_ref.1, f32[616,1232]{1,0:T(8,128)} %v_hbm.1, f32[616,256]{1,0:T(8,128)} %a_hbm.1), custom_call_target="tpu_custom_call" | custom-call | tf_op jit(solution)/shard_map/pallas_call | solution.py:276
  59.7 1.9 %copy.5 = f32[616,256]{1,0:T(8,128)} copy(f32[616,256]{1,0:T(8,128)} %shard_map.37) | data formatting | bytes 1261568

commit v3 on v2

--- a/solution.py
+++ b/solution.py
@@ -9,7 +9,8 @@
 
 LANES = 128
 GROUP = 256
-LEAD = 1
+VMEM = 67043328
+LEAD = 0
 MESH = pl.DeviceIdType.MESH
 
 
@@ -19,6 +20,18 @@
         value = value + bit * (((index // bit) % 2 + (mask // bit) % 2) % 2)
         bit *= 2
     return value
+
+
+def chunk_plan(n_col, halves):
+    plan = [(m, h) for m in reversed(range(n_col)) for h in range(halves)]
+    plan[2], plan[4] = plan[4], plan[2]
+    at = {chunk: t for t, chunk in enumerate(plan)}
+    parents = {}
+    for t, (mask, half) in enumerate(plan):
+        if mask:
+            low, high = mask & -mask, 1 << (mask.bit_length() - 1)
+            parents[t] = at[mask - (high if half % 2 == 0 else low), half]
+    return plan, parents
 
 
 def split(value):
@@ -44,8 +57,10 @@
     width = v_hbm.shape[1]
     per_group = GROUP // n_row
 
+    plan, parents = chunk_plan(n_col, halves)
+
     def chunk_owner(t):
-        return flipped(col, n_col - 1 - t // halves, n_col)
+        return flipped(col, plan[t][0], n_col)
 
     def load_v(at):
         return pltpu.make_async_copy(v_hbm.at[pl.ds(at * tile, tile)], v_buf, v_sem)
@@ -79,7 +94,7 @@
     def spread(t):
         peer = chunk_owner(t)
         return pltpu.make_async_remote_copy(
-            src_ref=pieces.at[peer, t % halves],
+            src_ref=pieces.at[peer, plan[t][1]],
             dst_ref=blocks.at[t, row],
             send_sem=spread_sem.at[t],
             recv_sem=block_sem.at[t, row],
@@ -89,7 +104,7 @@
 
     def keep(t):
         return pltpu.make_async_copy(
-            pieces.at[col, t % halves], blocks.at[t, row], block_sem.at[t, row]
+            pieces.at[col, t - away], blocks.at[t, row], block_sem.at[t, row]
         )
 
     def pass_on(t, block, sem, target, source=None):
@@ -116,7 +131,7 @@
     for t in range(away):
         spread(t).start()
     for t in range(away, chunks):
-        pass_own(t, pieces.at[col, t % halves])
+        pass_own(t, pieces.at[col, t - away])
         keep(t).start()
 
     lane = lax.broadcasted_iota(jnp.int32, (GROUP, GROUP), 1)
@@ -177,9 +192,17 @@
             dst_ref=arrived.at[t],
             send_sem=partial_send.at[t],
             recv_sem=partial_recv.at[t],
-            device_id=(row, chunk_owner(t)),
+            device_id=(row, flipped(col, plan[t][0] - plan[parents[t]][0], n_col)),
             device_id_type=MESH,
         )
+
+    def collect(t):
+        total = partial[t]
+        for child in range(t):
+            if parents.get(child) == t:
+                give(child).wait_recv()
+                total = total + arrived[child]
+        return total
 
     @pl.loop(0, chunks + LEAD + line - 1)
     def _(s):
@@ -233,17 +256,15 @@
                 await_block(done, j * 2 + (1 - core))
             multiply(done)
 
-            @pl.when(done < away)
-            def _():
-                give(done).start()
-
-    for t in range(away):
-        give(t).wait_recv()
+            for t in range(away):
+                @pl.when(done == t)
+                def _():
+                    if t in parents.values():
+                        partial[t] = collect(t)
+                    give(t).start()
+
     for h in range(halves):
-        total = partial[away + h]
-        for t in range(h, away, halves):
-            total = total + arrived[t]
-        out_ref[:, h * LANES:(h + 1) * LANES] = total
+        out_ref[:, h * LANES:(h + 1) * LANES] = collect(away + h)
 
     def await_sent(sem, count):
         sent = blocks.at[:, pl.ds(0, count)]
@@ -271,7 +292,9 @@
     depth = -(-width // GROUP) * GROUP
     tile = max(m for m in range(8, 641, 8) if rows % m == 0)
     tiles = rows // tile
-    spare = 4 * rows * own * 5 // 4
+    need = 4 * (tile * depth + rows * depth + depth * LANES + 3 * block * own)
+    need += 4 * LANES * chunks * (n_row * (rows_each + 8) + 2 * rows)
+    spare = max(0, min(4 * rows * own * 18, VMEM - need - (1 << 20)))
     dma = pltpu.SemaphoreType.DMA
     return pl.pallas_call(
         functools.partial(kernel, n_row, n_col, halves),
@@ -304,7 +327,7 @@
             dma((chunks - halves,)),
         ],
         compiler_params=pltpu.CompilerParams(
-            collective_id=0, has_side_effects=True, vmem_limit_bytes=67043328 - spare
+            collective_id=0, has_side_effects=True, vmem_limit_bytes=VMEM - spare
         ),
     )(phase_map, ladder_ints, amplitudes)
 

time: 61.8 us -> 56.4 us (0.913)
  Pallas kernels: 59.7 us -> 54.8 us
    pallas_call x1, Pallas kernels: 59.7 us -> 54.8 us  [per_device(): pl.pallas_call(functools.partial(kernel, n_row, n_col, halves), out_shape...]
    unnamed x1 -> x3, local copies, waits for them, and re-layouts: 1.95 us -> 1.49 us
where the time goes in v3:
time: 56.4 us; the launch traced here: 56.3 us
  Pallas kernels  54.8 us (97%)
  local copies, waits for them, and re-layouts  1.49 us (3%)
    pallas_call x1, Pallas kernels, per_device(): pl.pallas_call(functools.partial(kernel, n_row, n_col, halves), out_shape...  54.8 us
    unnamed x3, local copies, waits for them, and re-layouts  1.49 us

profile of v3, /device:TPU:0, one launch (start us, length us, event | category | flops | bytes accessed | tf_op | source)
XLA Modules:
  0.0 56.3 jit_solution(3032388012159973597)
XLA Ops:
  0.0 0.0 copy-start
  0.0 0.7 %copy-done = s32[8]{0:T(128)S(1)} copy-done((s32[8]{0:T(128)S(1)}, s32[8]{0:T(128)}, u32[]{:S(2)}) %copy-start) | copy-done | bytes 56
  0.7 54.8 %shard_map.37 = f32[616,256]{1,0:T(8,128)S(1)} custom-call(s32[8]{0:T(128)S(1)} %copy-done, f32[616,1232]{1,0:T(8,128)} %v_hbm.1, f32[616,256]{1,0:T(8,128)} %a_hbm.1), custom_call_target="tpu_custom_call" | custom-call | tf_op jit(solution)/shard_map/pallas_call | solution.py:299
  55.4 0.8 %copy.5 = f32[616,256]{1,0:T(8,128)} copy(f32[616,256]{1,0:T(8,128)S(1)} %shard_map.37) | data formatting | bytes 1261568
Async XLA Ops:
  0.0 0.7 %copy-start = (s32[8]{0:T(128)S(1)}, s32[8]{0:T(128)}, u32[]{:S(2)}) copy-start(s32[8]{0:T(128)} %phase_ref.1) | copy-start | bytes 100

commit v4 on v3

--- a/solution.py
+++ b/solution.py
@@ -214,7 +214,7 @@
         def _():
             pass_own(s)
 
-        @pl.when(s == LEAD)
+        @pl.when(s == 1)
         def _():
             for at in range(tiles):
                 if at:

time: 56.4 us -> 56.1 us (level)
  no operation moved by 1% of the time
where the time goes in v4:
time: 56.1 us; the launch traced here: 55.9 us
  Pallas kernels  54.4 us (97%)
  local copies, waits for them, and re-layouts  1.49 us (3%)
    pallas_call x1, Pallas kernels, per_device(): pl.pallas_call(functools.partial(kernel, n_row, n_col, halves), out_shape...  54.4 us
    unnamed x3, local copies, waits for them, and re-layouts  1.49 us

profile of v4, /device:TPU:0, one launch (start us, length us, event | category | flops | bytes accessed | tf_op | source)
XLA Modules:
  0.0 55.9 jit_solution(13174032368775794116)
XLA Ops:
  0.0 0.0 copy-start
  0.0 0.7 %copy-done = s32[8]{0:T(128)S(1)} copy-done((s32[8]{0:T(128)S(1)}, s32[8]{0:T(128)}, u32[]{:S(2)}) %copy-start) | copy-done | bytes 56
  0.7 54.4 %shard_map.37 = f32[616,256]{1,0:T(8,128)S(1)} custom-call(s32[8]{0:T(128)S(1)} %copy-done, f32[616,1232]{1,0:T(8,128)} %v_hbm.1, f32[616,256]{1,0:T(8,128)} %a_hbm.1), custom_call_target="tpu_custom_call" | custom-call | tf_op jit(solution)/shard_map/pallas_call | solution.py:299
  55.1 0.8 %copy.5 = f32[616,256]{1,0:T(8,128)} copy(f32[616,256]{1,0:T(8,128)S(1)} %shard_map.37) | data formatting | bytes 1261568
Async XLA Ops:
  0.0 0.7 %copy-start = (s32[8]{0:T(128)S(1)}, s32[8]{0:T(128)}, u32[]{:S(2)}) copy-start(s32[8]{0:T(128)} %phase_ref.1) | copy-start | bytes 100
